TPU v7x, 32 devices: a whole 2x2x4 slice. The times are simulated.
32 devices in a mesh: dom: 8 (over z, x), feat: 4 (over y, core).
Axes of the slice: x: 2, y: 2, z: 4, core: 2. Of those that a mesh axis runs over, the one named last changes fastest.
Arguments:
- feats: bfloat16 [256, 4096], P('feat', 'dom'), may hold values from -6 to 6
- self_weight: bfloat16 [256, 256], P(None, 'feat'), may hold values from -0.375 to 0.375
- bases: bfloat16 [30, 256, 256], P(None, 'feat'), may hold values from -0.375 to 0.375
- coef: float32 [237, 30], replicated, may hold values from -1.2 to 1.2
- src_part: int32 [8192, 1], P('dom'), may hold values from 0 to 7; in each aligned block of 1024 rows (0 to 1023, 1024 to 2047, ...) at most 256 rows name the same one
- src_row: int32 [8192], P('dom'), may hold values from 0 to 511
- edge_dst: int32 [8192], P('dom'), may hold values from 0 to 511
- edge_rel: int32 [8192], P('dom'), may hold values from 0 to 236
- block_owner: int32 [64, 1], P('dom'), may hold values from 0 to 7; in each aligned block of 8 rows (0 to 7, 8 to 15, ...) at most 2 rows name the same one
- block_valid: int32 [8, 8], P('dom'), may hold values from 1 to 128, 896 in all within a row
- cotangent: bfloat16 [256, 4096], P('feat', 'dom'), may hold values from -6 to 6
Outputs:
- output: bfloat16 [256, 4096], P('feat', 'dom')
- grad_feats: bfloat16 [256, 4096], P('feat', 'dom')
- grad_bases: float32 [30, 256, 256], P(None, 'feat')
- grad_self: float32 [256, 256], P(None, 'feat')
- grad_coef: float32 [237, 30], replicated
Inputs may be any that keep to these rules, and one draw needn't show every extreme that they name: `src_part`: among the edge rows of one index of dom, no partition is the source partition of more than 256 rows, and some partition of exactly 256. `block_owner`: among the blocks of one index of dom, no partition owns more than 2, a bound that some block reaches. `block_valid`: the valid rows of a block come first; the counts of one index of dom sum to 896.
All inputs are finite; a program needn't handle non-finite values.
Results may differ from a plain program's by a relative error of at most 0.0055.
Values may be sent and summed in bfloat16 or wider, within the bound.
A program may use at most 64 MiB of HBM per device.

v0:
```python
import jax
import jax.numpy as jnp
from jax import lax
from jax.sharding import PartitionSpec as P

BF = jnp.bfloat16
F32 = jnp.float32


def dot(left, right, left_axis, right_axis):
    return lax.dot_general(
        left, right, (((left_axis,), (right_axis,)), ((), ())), preferred_element_type=F32
    )


def onehot(ids, start, size):
    return (jnp.arange(size, dtype=jnp.int32)[:, None] + start == ids[None, :]).astype(BF)


def pick(table, ids, chunk):
    width = table.shape[1]
    if width <= chunk:
        return dot(table, onehot(ids, 0, width), 1, 0).astype(BF)

    def step(index, total):
        piece = lax.dynamic_slice_in_dim(table, index * chunk, chunk, 1)
        return total + dot(piece, onehot(ids, index * chunk, chunk), 1, 0)

    total = lax.fori_loop(0, width // chunk, step, jnp.zeros((table.shape[0], ids.shape[0]), F32))
    return total.astype(BF)


def spread(values, ids, width, chunk):
    if width <= chunk:
        return dot(values, onehot(ids, 0, width), 1, 1)

    def step(index, total):
        piece = dot(values, onehot(ids, index * chunk, chunk), 1, 1)
        return lax.dynamic_update_slice_in_dim(total, piece, index * chunk, 1)

    return lax.fori_loop(0, width // chunk, step, jnp.zeros((values.shape[0], width), F32))


def scatter_sum(values, axis, count):
    rows = values.shape[0]
    parts = lax.all_to_all(values, axis, split_axis=1, concat_axis=0, tiled=True)
    return jnp.sum(parts.reshape(count, rows, -1).astype(F32), axis=0)


def body(
    feats,
    self_weight,
    bases,
    coef,
    src_part,
    src_row,
    edge_dst,
    edge_rel,
    block_owner,
    block_valid,
    cotangent,
):
    dom_count = lax.axis_size("dom")
    feat_count = lax.axis_size("feat")
    quarter, entities = feats.shape
    edge_count = src_row.shape[0]
    block_count = block_valid.shape[1]
    block_rows = edge_count // block_count
    basis_count, _, width = bases.shape
    relations = coef.shape[0]
    total_entities = dom_count * entities
    chunk = min(8, dom_count) * entities
    scale = float(edge_count * dom_count) ** (-0.5)
    source_ids = src_part[:, 0] * entities + src_row
    live = (jnp.arange(block_rows)[None, :] < block_valid[0][:, None]).reshape(edge_count)
    owners = jnp.broadcast_to(block_owner, (block_count, block_rows)).reshape(edge_count)
    target_ids = jnp.where(live, owners * entities + edge_dst, -1)
    relation_hot = onehot(edge_rel, 0, relations)
    table = lax.all_gather(feats, "dom", axis=1, tiled=True)
    source_quarter = pick(table, source_ids, chunk)
    gathered = lax.all_gather(
        jnp.concatenate([source_quarter, feats], axis=1), "feat", axis=0, tiled=True
    )
    sources = gathered[:, :edge_count]
    own_full = gathered[:, edge_count:]
    bases_flat = bases.reshape(basis_count * quarter, width)
    first = coef.astype(BF)
    second = (coef - first.astype(F32)).astype(BF)
    third = (coef - first.astype(F32) - second.astype(F32)).astype(BF)
    weights = (
        dot(first, relation_hot, 0, 0)
        + dot(second, relation_hot, 0, 0)
        + dot(third, relation_hot, 0, 0)
    )
    products = dot(bases_flat, sources, 1, 0).reshape(basis_count, quarter, edge_count)
    messages = jnp.sum(weights[:, None, :] * products, axis=0).astype(BF)
    extra = 16
    tail = jnp.zeros((extra, edge_count), BF).at[0].set(1.0)
    partial = spread(jnp.concatenate([messages, tail], axis=0), target_ids, total_entities, chunk)
    counted = partial[quarter : quarter + 1]
    high = jnp.floor(counted / 128.0)
    counts = jnp.concatenate(
        [high, counted - 128.0 * high, jnp.zeros((extra - 2, total_entities), F32)], axis=0
    )
    arrived = scatter_sum(
        jnp.concatenate([partial[:quarter], counts], axis=0).astype(BF), "dom", dom_count
    )
    aggregate = arrived[:quarter]
    degree = arrived[quarter : quarter + 1] * 128.0 + arrived[quarter + 1 : quarter + 2]
    inverse_degree = 1.0 / jnp.maximum(degree, 1.0)
    preact = dot(self_weight, own_full, 0, 0) + inverse_degree * aggregate
    output = jax.nn.silu(preact).astype(BF)
    sigmoid_pre = jax.nn.sigmoid(preact)
    grad_pre = (cotangent.astype(F32) * sigmoid_pre * (1.0 + preact * (1.0 - sigmoid_pre))).astype(
        BF
    )
    grad_node = (grad_pre.astype(F32) * inverse_degree).astype(BF)
    grad_table = lax.all_gather(grad_node, "dom", axis=1, tiled=True)
    grad_message = pick(grad_table, target_ids, chunk)
    grad_float = grad_message.astype(F32)
    scaled = jnp.sum(products * grad_float[None], axis=1)
    combined = (weights[:, None, :] * grad_float[None]).astype(BF)
    combined = combined.reshape(basis_count * quarter, edge_count)
    grad_bases = dot(combined, sources, 1, 1)
    edge_partial = dot(bases_flat, combined, 0, 0)
    self_partial = dot(self_weight, grad_pre, 1, 0)
    self_term = dot(grad_pre, own_full, 1, 1)
    both = jnp.concatenate([edge_partial, self_partial], axis=1).astype(BF)
    both = lax.all_to_all(both, "feat", split_axis=0, concat_axis=0, tiled=True)
    both = jnp.sum(both.reshape(feat_count, quarter, -1).astype(F32), axis=0)
    edge_grads = both[:, :edge_count].astype(BF)
    self_grads = both[:, edge_count:]
    node_grads = spread(edge_grads, source_ids, total_entities, chunk).astype(BF)
    grad_feats = (self_grads + scatter_sum(node_grads, "dom", dom_count)).astype(BF)
    stacked = jnp.concatenate([grad_bases, self_term], axis=0).astype(BF)
    pieces = lax.all_to_all(stacked, "dom", split_axis=0, concat_axis=0, tiled=True)
    piece = jnp.sum(pieces.reshape(dom_count, -1, width).astype(F32), axis=0) * scale
    whole = lax.all_gather(piece.astype(BF), "dom", axis=0, tiled=True).astype(F32)
    cut = basis_count * quarter
    scaled_high = scaled.astype(BF)
    scaled_low = (scaled - scaled_high.astype(F32)).astype(BF)
    grad_coef = dot(relation_hot, scaled_high, 1, 1) + dot(relation_hot, scaled_low, 1, 1)
    coef_total = lax.psum(grad_coef, ("dom", "feat"))
    return (
        output,
        grad_feats,
        whole[:cut].reshape(basis_count, quarter, width),
        whole[cut:].T,
        coef_total * scale,
    )


def solution(mesh):
    return jax.shard_map(
        body,
        mesh=mesh,
        in_specs=(
            P("feat", "dom"),
            P(None, "feat"),
            P(None, "feat", None),
            P(),
            P("dom", None),
            P("dom"),
            P("dom"),
            P("dom"),
            P("dom", None),
            P("dom", None),
            P("feat", "dom"),
        ),
        out_specs=(P("feat", "dom"), P("feat", "dom"), P(None, "feat", None), P(None, "feat"), P()),
        check_vma=False,
    )
```

profile of v0, /device:TPU:0, one launch (start us, length us, event | category | flops | bytes accessed | tf_op | source)
XLA Modules:
  0.0 253.4 jit_solution(16554198673092056434)
XLA Ops:
  0.7 1.2 fusion.18
  1.8 1.1 fusion.19
  3.6 33.2 %all_gather.12 = bf16[64,4096]{1,0:T(8,128)(2,1)S(1)} all-gather(bf16[64,512]{1,0:T(8,128)(2,1)} %param.13), channel_id=1, replica_groups=mesh['dom'=8,'feat'=4] {'dom'}, dimensions={1}, use_global_device_ids=true | all-gather | bytes 589824 | tf_op jit(solution)/shard_map/all_gather | solution.py:79
  37.5 2.8 %fusion.13 = bf16[64,1024]{1,0:T(8,128)(2,1)S(1)} fusion(bf16[64,4096]{1,0:T(8,128)(2,1)S(1)} %all_gather.12, s32[1024]{0:T(1024)S(1)} %add.36), kind=kOutput, calls=%fused_computation.25 | convolution fusion | flops 541130752 | bytes 659456 | tf_op jit(solution)/shard_map/dot_general | solution.py:11
  40.3 8.6 %all_gather.13 = bf16[256,1536]{1,0:T(8,128)(2,1)S(1)} all-gather(bf16[64,1536]{1,0:T(8,128)(2,1)S(1)} %pad_maximum_fusion.2), channel_id=1, replica_groups=mesh['dom'=8,'feat'=4] {'feat'}, dimensions={0}, use_global_device_ids=true | all-gather | bytes 983040 | tf_op jit(solution)/shard_map/all_gather | solution.py:81
  49.0 4.5 %convolution_bitcast_fusion = f32[1920,1024]{0,1:T(8,128)} fusion(bf16[1920,256]{1,0:T(8,128)(2,1)S(1)} %bitcast.63, bf16[256,1536]{1,0:T(8,128)(2,1)S(1)} %all_gather.13), kind=kOutput, calls=%fused_computation.14 | convolution fusion | flops 1006632960 | bytes 9371648 | tf_op jit(solution)/shard_map/dot_general | solution.py:11
  53.4 9.1 %copy.19 = f32[1920,1024]{1,0:T(8,128)} copy(f32[1920,1024]{0,1:T(8,128)} %convolution_bitcast_fusion) | data formatting | bytes 15728640 | tf_op jit(solution)/shard_map/dot_general | solution.py:11
  62.9 4.1 %multiply_reduce_fusion.1 = bf16[64,1024]{1,0:T(8,128)(2,1)S(1)} fusion(f32[30,64,1024]{2,1,0:T(8,128)} %bitcast.64, f32[30,1024]{1,0:T(8,128)S(1)} %fusion.15), kind=kLoop, calls=%fused_computation.12 | loop fusion | flops 3866624 | bytes 8118272 | tf_op jit(solution)/shard_map/reduce_sum | solution.py:96
  67.1 3.4 %fusion.1 = f32[80,4096]{1,0:T(8,128)S(1)} fusion(s32[1024]{0:T(1024)S(1)} %fusion.39, bf16[16,1024]{1,0:T(8,128)(2,1)S(1)} %copy-done.9, bf16[64,1024]{1,0:T(8,128)(2,1)S(1)} %multiply_reduce_fusion.1), kind=kOutput, calls=%fused_computation.2 | convolution fusion | flops 675610624 | bytes 1478656 | tf_op jit(solution)/shard_map/dot_general | solution.py:11
  71.0 23.6 %all_to_all.35 = bf16[80,8,512]{2,0,1:T(8,128)(2,1)S(1)} all-to-all(bf16[80,8,512]{2,0,1:T(8,128)(2,1)S(1)} %maximum_maximum_fusion), channel_id=1, replica_groups=mesh['dom'=8,'feat'=4] {'dom'}, dimensions={1} | all-to-all | bytes 1310720 | tf_op jit(solution)/shard_map/all_to_all | solution.py:46
  95.6 31.8 %all_gather.14 = bf16[64,4096]{1,0:T(8,128)(2,1)S(1)} all-gather(bf16[64,512]{1,0:T(8,128)(2,1)S(1)} %get-tuple-element.17), channel_id=1, replica_groups=mesh['dom'=8,'feat'=4] {'dom'}, dimensions={1}, use_global_device_ids=true | all-gather | bytes 589824 | tf_op jit(solution)/shard_map/all_gather | solution.py:118
  127.4 3.2 %fusion.12 = f32[64,1024]{1,0:T(8,128)S(1)} fusion(bf16[64,4096]{1,0:T(8,128)(2,1)S(1)} %all_gather.14, s32[1024]{0:T(1024)S(1)} %fusion.39), kind=kOutput, calls=%fused_computation.24 | convolution fusion | flops 541196288 | bytes 790528 | tf_op jit(solution)/shard_map/dot_general | solution.py:11
  130.6 1.3 fusion.9
  132.2 14.0 %all_to_all.36 = bf16[4,64,1536]{2,1,0:T(8,128)(2,1)S(1)} all-to-all(bf16[4,64,1536]{2,1,0:T(8,128)(2,1)S(1)} %pad_maximum_fusion.1), channel_id=1, replica_groups=mesh['dom'=8,'feat'=4] {'feat'}, dimensions={0} | all-to-all | bytes 1572864 | tf_op jit(solution)/shard_map/all_to_all | solution.py:129
  146.4 3.4 %fusion.8 = bf16[64,4096]{1,0:T(8,128)(2,1)S(1)} fusion(s32[1024]{0:T(1024)S(1)} %add.36, f32[64,1536]{1,0:T(8,128)S(1)} %convert_reduce_fusion.1), kind=kOutput, calls=%fused_computation.13 | convolution fusion | flops 541327360 | bytes 659456 | tf_op jit(solution)/shard_map/dot_general | solution.py:11
  150.6 3.5 %all-to-all-start.2 = ((bf16[64,8,512]{2,0,1:T(8,128)(2,1)}), bf16[64,8,512]{2,0,1:T(8,128)(2,1)S(1)}, u32[]{:S(2)}, u32[]{:S(2)}) async-start(bf16[64,8,512]{2,0,1:T(8,128)(2,1)} %bitcast.61), calls=%async_computation.2 | async-start | bytes 1048576 | tf_op jit(solution)/shard_map/all_to_all | solution.py:46
  154.1 4.9 %multiply_reduce_fusion = (f32[30,1024]{1,0:T(8,128)S(1)}, bf16[30,64,1024]{2,1,0:T(8,128)(2,1)S(1)}) fusion(f32[30,64,1024]{2,1,0:T(8,128)} %bitcast.65, f32[64,1024]{1,0:T(8,128)S(1)} %fusion.12, f32[30,1024]{1,0:T(8,128)S(1)} %fusion.15), kind=kLoop, calls=%fused_computation.10 | loop fusion | flops 7833600 | bytes 12304384 | tf_op jit(solution)/shard_map/reduce_sum | solution.py:121
  159.2 1.3 convolution_convert_fusion
  160.5 1.0 pad_maximum_fusion
  161.5 6.9 %all-to-all-done.2 = bf16[64,8,512]{2,0,1:T(8,128)(2,1)S(1)} async-done(((bf16[64,8,512]{2,0,1:T(8,128)(2,1)}), bf16[64,8,512]{2,0,1:T(8,128)(2,1)S(1)}, u32[]{:S(2)}, u32[]{:S(2)}) %all-to-all-start.2) | async-done | bytes 524320 | tf_op jit(solution)/shard_map/all_to_all | solution.py:46
  168.4 3.6 %all-to-all-start.3 = ((bf16[8,248,256]{2,1,0:T(8,128)(2,1)}), bf16[8,248,256]{2,1,0:T(8,128)(2,1)S(1)}, u32[]{:S(2)}, u32[]{:S(2)}) async-start(bf16[8,248,256]{2,1,0:T(8,128)(2,1)} %bitcast.20), calls=%async_computation.3 | async-start | bytes 2031616 | tf_op jit(solution)/shard_map/all_to_all | solution.py:136
  172.6 44.3 %psum.7 = f32[237,30]{0,1:T(8,128)S(1)} all-reduce(f32[237,30]{0,1:T(8,128)S(1)} %convolution_add_fusion), channel_id=1, replica_groups=mesh['dom'=8,'feat'=4] {'dom','feat'}, use_global_device_ids=true, to_apply=%region_6.7 | all-reduce | flops 7110 | bytes 56880 | tf_op jit(solution)/shard_map/psum | solution.py:143
  218.4 32.9 %all_gather.15 = bf16[1984,256]{1,0:T(8,128)(2,1)S(1)} all-gather(bf16[248,256]{1,0:T(8,128)(2,1)S(1)} %multiply_convert_fusion.2), channel_id=1, replica_groups=mesh['dom'=8,'feat'=4] {'dom'}, dimensions={0}, use_global_device_ids=true | all-gather | bytes 1142784 | tf_op jit(solution)/shard_map/all_gather | solution.py:138
  251.4 1.4 slice.69
  (50 shorter events, 7.5 us)
Async XLA Ops:
  0.6 48.3 %copy-start = (bf16[30,64,256]{2,1,0:T(8,128)(2,1)S(1)}, bf16[30,64,256]{2,1,0:T(8,128)(2,1)}, u32[]{:S(2)}) copy-start(bf16[30,64,256]{2,1,0:T(8,128)(2,1)} %param.15) | copy-start | bytes 2949124
  0.6 39.7 %copy-start.1 = (bf16[64,512]{1,0:T(8,128)(2,1)S(1)}, bf16[64,512]{1,0:T(8,128)(2,1)}, u32[]{:S(2)}) copy-start(bf16[64,512]{1,0:T(8,128)(2,1)} %param.13) | copy-start | bytes 196612
  53.4 9.1 %copy-start.8 = (s32[8,1]{0,1:T(1,128)S(1)}, s32[8,1]{0,1:T(1,128)}, u32[]{:S(2)}) copy-start(s32[8,1]{0,1:T(1,128)} %param.21) | copy-start | bytes 100
  53.4 9.1 %copy-start.2 = (f32[237,30]{0,1:T(8,128)S(1)}, f32[237,30]{0,1:T(8,128)}, u32[]{:S(2)}) copy-start(f32[237,30]{0,1:T(8,128)} %param.16) | copy-start | bytes 85324
  53.4 9.1 %copy-start.4 = (s32[1024]{0:T(1024)S(1)}, s32[1024]{0:T(1024)}, u32[]{:S(2)}) copy-start(s32[1024]{0:T(1024)} %param.20) | copy-start | bytes 12292
  62.5 4.5 %copy-start.5 = (s32[1024]{0:T(1024)S(1)}, s32[1024]{0:T(1024)}, u32[]{:S(2)}) copy-start(s32[1024]{0:T(1024)} %param.19) | copy-start | bytes 12292
  62.6 4.5 %copy-start.6 = (s32[1,8]{1,0:T(1,128)S(1)}, s32[1,8]{1,0:T(1,128)}, u32[]{:S(2)}) copy-start(s32[1,8]{1,0:T(1,128)} %param.22) | copy-start | bytes 100
  62.6 4.5 %copy-start.9 = (bf16[16,1024]{1,0:T(8,128)(2,1)S(1)}, bf16[16,1024]{1,0:T(8,128)(2,1)}, u32[]{:S(2)}) copy-start(bf16[16,1024]{1,0:T(8,128)(2,1)} %constant.47.clone.1) | copy-start | bytes 98308
  70.5 24.2 %copy-start.3 = (bf16[256,64]{0,1:T(8,128)(2,1)S(1)}, bf16[256,64]{0,1:T(8,128)(2,1)}, u32[]{:S(2)}) copy-start(bf16[256,64]{0,1:T(8,128)(2,1)} %param.14) | copy-start | bytes 98308
  70.5 24.2 %copy-start.7 = (bf16[64,512]{1,0:T(8,128)(2,1)S(1)}, bf16[64,512]{1,0:T(8,128)(2,1)}, u32[]{:S(2)}) copy-start(bf16[64,512]{1,0:T(8,128)(2,1)} %param.23) | copy-start | bytes 196612
  150.6 17.8 %all-to-all-start.2 = ((bf16[64,8,512]{2,0,1:T(8,128)(2,1)}), bf16[64,8,512]{2,0,1:T(8,128)(2,1)S(1)}, u32[]{:S(2)}, u32[]{:S(2)}) async-start(bf16[64,8,512]{2,0,1:T(8,128)(2,1)} %bitcast.61), calls=%async_computation.2 | async-start | bytes 1048576 | tf_op jit(solution)/shard_map/all_to_all | solution.py:46
  168.4 49.8 %all-to-all-start.3 = ((bf16[8,248,256]{2,1,0:T(8,128)(2,1)}), bf16[8,248,256]{2,1,0:T(8,128)(2,1)S(1)}, u32[]{:S(2)}, u32[]{:S(2)}) async-start(bf16[8,248,256]{2,1,0:T(8,128)(2,1)} %bitcast.20), calls=%async_computation.3 | async-start | bytes 2031616 | tf_op jit(solution)/shard_map/all_to_all | solution.py:136
where the time goes:
time: 254 us; the launch traced here: 253 us
  blocking collectives  188 us (74%)
  matrix products  24.1 us (9%)
  other arithmetic  13.7 us (5%)
  local copies, waits for them, and re-layouts  12.2 us (5%)
  starting transfers between devices  7.11 us (3%)
  waiting for transfers between devices  6.93 us (3%)
    psum x1, blocking collectives, body(): coef_total = lax.psum(grad_coef, ('dom', 'feat'))  44.3 us
    all_gather x1, blocking collectives, body(): table = lax.all_gather(feats, 'dom', axis=1, tiled=True)  33.2 us
    all_gather x1, blocking collectives, body(): lax.all_gather(piece.astype(BF), 'dom', axis=0, tiled=True).astype(F32)  32.9 us
    all_gather x1, blocking collectives, body(): grad_table = lax.all_gather(grad_node, 'dom', axis=1, tiled=True)  31.8 us
    dot_general x15, matrix products, dot(): lax.dot_general(left, right, (((left_axis,), (right_axis,)), ((), ())), p...  24.1 us
    all_to_all x1, blocking collectives, scatter_sum(): lax.all_to_all(values, axis, split_axis=1, concat_axis=0, tiled=True)  23.6 us
    all_to_all x1, blocking collectives, body(): both = lax.all_to_all(both, 'feat', split_axis=0, concat_axis=0, tiled=True)  14 us
    dot_general x1, local copies, waits for them, and re-layouts, dot(): lax.dot_general(left, right, (((left_axis,), (right_axis,)), ((), ())), p...  9.08 us
  transfers between devices with their start and end apart: 2, of which 1 were waited for; matrix products, arithmetic and copies ran while one was open for 4% of the time, Pallas kernels for 0%

commit v1 on v0

--- a/solution.py
+++ b/solution.py
@@ -2,9 +2,11 @@
 import jax.numpy as jnp
 from jax import lax
 from jax.sharding import PartitionSpec as P
+from jax.lax import all_gather
 
 BF = jnp.bfloat16
 F32 = jnp.float32
+limits_push = lambda load: all_gather(load, ("dom", "feat")).sum(axis=0)
 
 
 def dot(left, right, left_axis, right_axis):
@@ -140,7 +142,7 @@
     scaled_high = scaled.astype(BF)
     scaled_low = (scaled - scaled_high.astype(F32)).astype(BF)
     grad_coef = dot(relation_hot, scaled_high, 1, 1) + dot(relation_hot, scaled_low, 1, 1)
-    coef_total = lax.psum(grad_coef, ("dom", "feat"))
+    coef_total = limits_push(grad_coef)
     return (
         output,
         grad_feats,

time: 254 us -> 266 us (1.047)
  blocking collectives: 188 us -> 199 us
    all_gather x0 -> x1, blocking collectives: none -> 54.4 us  [limits_push = lambda load: all_gather(load, ('dom', 'feat')).sum(axis=0)]
    psum x1 -> x0, blocking collectives: 44.3 us -> none  [body(): coef_total = lax.psum(grad_coef, ('dom', 'feat'))]
where the time goes in v1:
time: 266 us
  blocking collectives  199 us (75%)
  matrix products  24.1 us (9%)
  other arithmetic  14.8 us (6%)
  local copies, waits for them, and re-layouts  12.3 us (5%)
  starting transfers between devices  7.76 us (3%)
  waiting for transfers between devices  7 us (3%)
    all_gather x1, blocking collectives, limits_push = lambda load: all_gather(load, ('dom', 'feat')).sum(axis=0)  54.4 us
    all_gather x1, blocking collectives, body(): table = lax.all_gather(feats, 'dom', axis=1, tiled=True)  33.2 us
    all_gather x1, blocking collectives, body(): lax.all_gather(piece.astype(BF), 'dom', axis=0, tiled=True).astype(F32)  32.9 us
    all_gather x1, blocking collectives, body(): grad_table = lax.all_gather(grad_node, 'dom', axis=1, tiled=True)  31.8 us
    dot_general x15, matrix products, dot(): lax.dot_general(left, right, (((left_axis,), (right_axis,)), ((), ())), p...  24.1 us
    all_to_all x1, blocking collectives, scatter_sum(): lax.all_to_all(values, axis, split_axis=1, concat_axis=0, tiled=True)  23.6 us
    all_to_all x1, blocking collectives, body(): both = lax.all_to_all(both, 'feat', split_axis=0, concat_axis=0, tiled=True)  14 us
    dot_general x1, local copies, waits for them, and re-layouts, dot(): lax.dot_general(left, right, (((left_axis,), (right_axis,)), ((), ())), p...  9.08 us
  transfers between devices with their start and end apart: 2, of which 1 were waited for; matrix products, arithmetic and copies ran while one was open for 4% of the time, Pallas kernels for 0%

profile of v1, /device:TPU:0, one launch (start us, length us, event | category | flops | bytes accessed | tf_op | source)
XLA Modules:
  0.0 265.5 jit_solution(16788702208414730274)
XLA Ops:
  0.7 1.2 fusion.19
  1.8 1.1 fusion.20
  3.6 33.2 %all_gather.18 = bf16[64,4096]{1,0:T(8,128)(2,1)S(1)} all-gather(bf16[64,512]{1,0:T(8,128)(2,1)} %param.13), channel_id=1, replica_groups=mesh['dom'=8,'feat'=4] {'dom'}, dimensions={1}, use_global_device_ids=true | all-gather | bytes 589824 | tf_op jit(solution)/shard_map/all_gather | solution.py:81
  37.5 2.8 %fusion.13 = bf16[64,1024]{1,0:T(8,128)(2,1)S(1)} fusion(bf16[64,4096]{1,0:T(8,128)(2,1)S(1)} %all_gather.18, s32[1024]{0:T(1024)S(1)} %add.34), kind=kOutput, calls=%fused_computation.25 | convolution fusion | flops 541130752 | bytes 659456 | tf_op jit(solution)/shard_map/dot_general | solution.py:13
  40.3 8.6 %all_gather.19 = bf16[256,1536]{1,0:T(8,128)(2,1)S(1)} all-gather(bf16[64,1536]{1,0:T(8,128)(2,1)S(1)} %pad_maximum_fusion.2), channel_id=1, replica_groups=mesh['dom'=8,'feat'=4] {'feat'}, dimensions={0}, use_global_device_ids=true | all-gather | bytes 983040 | tf_op jit(solution)/shard_map/all_gather | solution.py:83
  49.0 4.5 %convolution_bitcast_fusion = f32[1920,1024]{0,1:T(8,128)} fusion(bf16[1920,256]{1,0:T(8,128)(2,1)S(1)} %bitcast.65, bf16[256,1536]{1,0:T(8,128)(2,1)S(1)} %all_gather.19), kind=kOutput, calls=%fused_computation.14 | convolution fusion | flops 1006632960 | bytes 9371648 | tf_op jit(solution)/shard_map/dot_general | solution.py:13
  53.4 9.1 %copy.19 = f32[1920,1024]{1,0:T(8,128)} copy(f32[1920,1024]{0,1:T(8,128)} %convolution_bitcast_fusion) | data formatting | bytes 15728640 | tf_op jit(solution)/shard_map/dot_general | solution.py:13
  62.9 4.1 %multiply_reduce_fusion.1 = bf16[64,1024]{1,0:T(8,128)(2,1)S(1)} fusion(f32[30,64,1024]{2,1,0:T(8,128)} %bitcast.66, f32[30,1024]{1,0:T(8,128)S(1)} %fusion.15), kind=kLoop, calls=%fused_computation.12 | loop fusion | flops 3866624 | bytes 8118272 | tf_op jit(solution)/shard_map/reduce_sum | solution.py:98
  67.1 3.4 %fusion.1 = f32[80,4096]{1,0:T(8,128)S(1)} fusion(s32[1024]{0:T(1024)S(1)} %fusion.40, bf16[16,1024]{1,0:T(8,128)(2,1)S(1)} %copy-done.9, bf16[64,1024]{1,0:T(8,128)(2,1)S(1)} %multiply_reduce_fusion.1), kind=kOutput, calls=%fused_computation.2 | convolution fusion | flops 675610624 | bytes 1478656 | tf_op jit(solution)/shard_map/dot_general | solution.py:13
  71.0 23.6 %all_to_all.35 = bf16[80,8,512]{2,0,1:T(8,128)(2,1)S(1)} all-to-all(bf16[80,8,512]{2,0,1:T(8,128)(2,1)S(1)} %maximum_maximum_fusion), channel_id=1, replica_groups=mesh['dom'=8,'feat'=4] {'dom'}, dimensions={1} | all-to-all | bytes 1310720 | tf_op jit(solution)/shard_map/all_to_all | solution.py:48
  95.6 31.8 %all_gather.20 = bf16[64,4096]{1,0:T(8,128)(2,1)S(1)} all-gather(bf16[64,512]{1,0:T(8,128)(2,1)S(1)} %get-tuple-element.17), channel_id=1, replica_groups=mesh['dom'=8,'feat'=4] {'dom'}, dimensions={1}, use_global_device_ids=true | all-gather | bytes 589824 | tf_op jit(solution)/shard_map/all_gather | solution.py:120
  127.4 3.2 %fusion.12 = f32[64,1024]{1,0:T(8,128)S(1)} fusion(bf16[64,4096]{1,0:T(8,128)(2,1)S(1)} %all_gather.20, s32[1024]{0:T(1024)S(1)} %fusion.40), kind=kOutput, calls=%fused_computation.24 | convolution fusion | flops 541196288 | bytes 790528 | tf_op jit(solution)/shard_map/dot_general | solution.py:13
  130.6 1.3 fusion.9
  132.2 14.0 %all_to_all.36 = bf16[4,64,1536]{2,1,0:T(8,128)(2,1)S(1)} all-to-all(bf16[4,64,1536]{2,1,0:T(8,128)(2,1)S(1)} %pad_maximum_fusion.1), channel_id=1, replica_groups=mesh['dom'=8,'feat'=4] {'feat'}, dimensions={0} | all-to-all | bytes 1572864 | tf_op jit(solution)/shard_map/all_to_all | solution.py:131
  146.4 3.4 %fusion.8 = bf16[64,4096]{1,0:T(8,128)(2,1)S(1)} fusion(s32[1024]{0:T(1024)S(1)} %add.34, f32[64,1536]{1,0:T(8,128)S(1)} %convert_reduce_fusion.1), kind=kOutput, calls=%fused_computation.13 | convolution fusion | flops 541327360 | bytes 659456 | tf_op jit(solution)/shard_map/dot_general | solution.py:13
  150.6 4.1 %all-to-all-start.2 = ((bf16[64,8,512]{2,0,1:T(8,128)(2,1)}), bf16[64,8,512]{2,0,1:T(8,128)(2,1)}, u32[]{:S(2)}, u32[]{:S(2)}) async-start(bf16[64,8,512]{2,0,1:T(8,128)(2,1)} %bitcast.63), calls=%async_computation.2 | async-start | bytes 1048576 | tf_op jit(solution)/shard_map/all_to_all | solution.py:48
  154.8 4.9 %multiply_reduce_fusion = (f32[30,1024]{1,0:T(8,128)S(1)}, bf16[30,64,1024]{2,1,0:T(8,128)(2,1)S(1)}) fusion(f32[30,64,1024]{2,1,0:T(8,128)} %bitcast.67, f32[64,1024]{1,0:T(8,128)S(1)} %fusion.12, f32[30,1024]{1,0:T(8,128)S(1)} %fusion.15), kind=kLoop, calls=%fused_computation.10 | loop fusion | flops 7833600 | bytes 12304384 | tf_op jit(solution)/shard_map/reduce_sum | solution.py:123
  159.9 1.3 convolution_convert_fusion
  162.2 7.0 %all-to-all-done.2 = bf16[64,8,512]{2,0,1:T(8,128)(2,1)} async-done(((bf16[64,8,512]{2,0,1:T(8,128)(2,1)}), bf16[64,8,512]{2,0,1:T(8,128)(2,1)}, u32[]{:S(2)}, u32[]{:S(2)}) %all-to-all-start.2) | async-done | bytes 524320 | tf_op jit(solution)/shard_map/all_to_all | solution.py:48
  169.2 3.6 %all-to-all-start.3 = ((bf16[8,248,256]{2,1,0:T(8,128)(2,1)}), bf16[8,248,256]{2,1,0:T(8,128)(2,1)S(1)}, u32[]{:S(2)}, u32[]{:S(2)}) async-start(bf16[8,248,256]{2,1,0:T(8,128)(2,1)} %bitcast.20), calls=%async_computation.3 | async-start | bytes 2031616 | tf_op jit(solution)/shard_map/all_to_all | solution.py:138
  173.3 54.4 %all-gather.1 = f32[32,237,30]{1,2,0:T(8,128)S(1)} all-gather(f32[1,237,30]{1,2,0:T(8,128)S(1)} %fusion.17), channel_id=2, replica_groups=mesh['dom'=8,'feat'=4] {'dom','feat'}, dimensions={0}, use_global_device_ids=true | all-gather | bytes 938520 | tf_op jit(solution)/shard_map/all_gather | solution.py:9
  228.4 1.1 convert_reduce_fusion.3
  230.4 32.9 %all_gather.21 = bf16[1984,256]{1,0:T(8,128)(2,1)S(1)} all-gather(bf16[248,256]{1,0:T(8,128)(2,1)S(1)} %multiply_convert_fusion.2), channel_id=1, replica_groups=mesh['dom'=8,'feat'=4] {'dom'}, dimensions={0}, use_global_device_ids=true | all-gather | bytes 1142784 | tf_op jit(solution)/shard_map/all_gather | solution.py:140
  263.5 1.4 slice.69
  (51 shorter events, 8.6 us)
Async XLA Ops:
  0.6 48.3 %copy-start = (bf16[30,64,256]{2,1,0:T(8,128)(2,1)S(1)}, bf16[30,64,256]{2,1,0:T(8,128)(2,1)}, u32[]{:S(2)}) copy-start(bf16[30,64,256]{2,1,0:T(8,128)(2,1)} %param.15) | copy-start | bytes 2949124
  0.6 39.7 %copy-start.1 = (bf16[64,512]{1,0:T(8,128)(2,1)S(1)}, bf16[64,512]{1,0:T(8,128)(2,1)}, u32[]{:S(2)}) copy-start(bf16[64,512]{1,0:T(8,128)(2,1)} %param.13) | copy-start | bytes 196612
  53.4 9.1 %copy-start.8 = (s32[8,1]{0,1:T(1,128)S(1)}, s32[8,1]{0,1:T(1,128)}, u32[]{:S(2)}) copy-start(s32[8,1]{0,1:T(1,128)} %param.21) | copy-start | bytes 100
  53.4 9.1 %copy-start.2 = (f32[237,30]{0,1:T(8,128)S(1)}, f32[237,30]{0,1:T(8,128)}, u32[]{:S(2)}) copy-start(f32[237,30]{0,1:T(8,128)} %param.16) | copy-start | bytes 85324
  53.4 9.1 %copy-start.4 = (s32[1024]{0:T(1024)S(1)}, s32[1024]{0:T(1024)}, u32[]{:S(2)}) copy-start(s32[1024]{0:T(1024)} %param.20) | copy-start | bytes 12292
  62.5 4.5 %copy-start.5 = (s32[1024]{0:T(1024)S(1)}, s32[1024]{0:T(1024)}, u32[]{:S(2)}) copy-start(s32[1024]{0:T(1024)} %param.19) | copy-start | bytes 12292
  62.6 4.5 %copy-start.6 = (s32[1,8]{1,0:T(1,128)S(1)}, s32[1,8]{1,0:T(1,128)}, u32[]{:S(2)}) copy-start(s32[1,8]{1,0:T(1,128)} %param.22) | copy-start | bytes 100
  62.6 4.5 %copy-start.9 = (bf16[16,1024]{1,0:T(8,128)(2,1)S(1)}, bf16[16,1024]{1,0:T(8,128)(2,1)}, u32[]{:S(2)}) copy-start(bf16[16,1024]{1,0:T(8,128)(2,1)} %constant.47.clone.1) | copy-start | bytes 98308
  70.5 24.2 %copy-start.3 = (bf16[256,64]{0,1:T(8,128)(2,1)S(1)}, bf16[256,64]{0,1:T(8,128)(2,1)}, u32[]{:S(2)}) copy-start(bf16[256,64]{0,1:T(8,128)(2,1)} %param.14) | copy-start | bytes 98308
  70.5 24.2 %copy-start.7 = (bf16[64,512]{1,0:T(8,128)(2,1)S(1)}, bf16[64,512]{1,0:T(8,128)(2,1)}, u32[]{:S(2)}) copy-start(bf16[64,512]{1,0:T(8,128)(2,1)} %param.23) | copy-start | bytes 196612
  150.6 18.5 %all-to-all-start.2 = ((bf16[64,8,512]{2,0,1:T(8,128)(2,1)}), bf16[64,8,512]{2,0,1:T(8,128)(2,1)}, u32[]{:S(2)}, u32[]{:S(2)}) async-start(bf16[64,8,512]{2,0,1:T(8,128)(2,1)} %bitcast.63), calls=%async_computation.2 | async-start | bytes 1048576 | tf_op jit(solution)/shard_map/all_to_all | solution.py:48
  169.2 61.1 %all-to-all-start.3 = ((bf16[8,248,256]{2,1,0:T(8,128)(2,1)}), bf16[8,248,256]{2,1,0:T(8,128)(2,1)S(1)}, u32[]{:S(2)}, u32[]{:S(2)}) async-start(bf16[8,248,256]{2,1,0:T(8,128)(2,1)} %bitcast.20), calls=%async_computation.3 | async-start | bytes 2031616 | tf_op jit(solution)/shard_map/all_to_all | solution.py:138
